TPU v7x, 32 devices: a whole 2x2x4 slice. The times are simulated.
32 devices in a mesh: row: 8 (over y, x, core), col: 4 (over z).
Axes of the slice: x: 2, y: 2, z: 4, core: 2. Of those that a mesh axis runs over, the one named last changes fastest.
Arguments:
- species: float32 [2, 256, 256, 128], P(None, None, 'row', 'col'), may hold values from -6 to 6
- coupling: float32 [2, 2], replicated, may hold values from -4 to 4
- symbol_x: float32 [256], replicated, may hold values from 0.3 to 3
- symbol_y: float32 [256], replicated, may hold values from 0.3 to 3
- symbol_z: float32 [128], replicated, may hold values from 0.3 to 3
Outputs:
- modes: float32 [2, 256, 256, 128], P(None, 'row', 'col')
All inputs are finite; a program needn't handle non-finite values.
Results may differ from a plain program's by a relative error of at most 0.000078.
Values sent between devices are 32-bit elements.
A program may use at most 128 MiB of HBM per device.

v0:
```python
import functools

import jax
import jax.numpy as jnp
import numpy as np
from jax import lax
from jax.experimental import pallas as pl
from jax.experimental.pallas import tpu as pltpu
from jax.sharding import PartitionSpec as P

MESH = pl.DeviceIdType.MESH
LANES = 128
SUB = 8


def mode_table(count):
    rank = np.arange(1, count + 1)
    angle = np.pi / (count + 1) * ((rank[:, None] * rank[None, :]) % (2 * count + 2))
    return (np.sin(angle) * np.sqrt(2.0 / (count + 1))).astype(np.float32)


def halves_of(table):
    high = table.astype(jnp.bfloat16)
    low = (table - high.astype(np.float32)).astype(jnp.bfloat16)
    return high, low


def halves(values):
    high = values.astype(jnp.bfloat16)
    low = (values - high.astype(jnp.float32)).astype(jnp.bfloat16)
    return high, low


def partner(me, step, count):
    if count & (count - 1):
        return lax.rem(me + step, count)
    other, bit = me, 1
    while bit < count:
        if step & bit:
            other = other + bit * (1 - 2 * lax.rem(me // bit, 2))
        bit *= 2
    return other


def swap_groups(parts):
    parts = list(parts)
    count = len(parts)
    width = LANES // count
    lane = lax.broadcasted_iota(jnp.int32, parts[0].shape, 1)
    step = count // 2
    while step:
        keep = lax.rem(lane // (width * step), 2) == 0
        for first in range(count):
            if first & step:
                continue
            a, b = parts[first], parts[first + step]
            parts[first] = jnp.where(keep, a, pltpu.roll(b, width * step, 1))
            parts[first + step] = jnp.where(keep, pltpu.roll(a, LANES - width * step, 1), b)
        step //= 2
    return parts


def kernel(sizes, coupling_ref, sx_ref, a_hbm, hx_hbm, hy_hbm, hz_hbm, sy_ref, sz_ref, o_ref,
           a_ref, hx_ref, hy_ref, hz_ref, sy_rows, m_ref, t_ref, r_ref, v_ref, w_ref,
           load_a, load_h, send_row, recv_row, send_col, recv_col, own_row, own_col):
    rows, cols, fields, nx, ny, nz = sizes
    share_y = ny // cols
    groups = LANES // (nz // cols)
    blocks = ny // rows // groups
    chunks = nx // rows // SUB
    quads = SUB // groups
    total = fields * chunks
    slab = blocks * SUB
    row, col = lax.axis_index("row"), lax.axis_index("col")
    per_dot = 2
    width = per_dot * LANES
    pieces = blocks // per_dot

    def load(f, n):
        at = pl.ds(n * width, width)
        return pltpu.make_async_copy(a_hbm.at[f, at], a_ref.at[f, at], load_a.at[f, n])

    tables = [pltpu.make_async_copy(src, dst, load_h.at[n]) for n, (src, dst) in enumerate(
        ((hx_hbm, hx_ref), (hy_hbm, hy_ref), (hz_hbm, hz_ref)))]
    tables[0].start()
    for f in range(fields):
        for n in range(pieces):
            load(f, n).start()
    tables[1].start()
    tables[2].start()

    barrier = pltpu.get_barrier_semaphore()
    for step in range(1, rows):
        pl.semaphore_signal(barrier, inc=1, device_id={"row": partner(row, step, rows)}, device_id_type=MESH)
    for step in range(1, cols):
        pl.semaphore_signal(barrier, inc=1, device_id={"col": partner(col, step, cols)}, device_id_type=MESH)

    def row_copy(i, step):
        to = partner(row, step, rows)
        return pltpu.make_async_remote_copy(
            src_ref=t_ref.at[i, to], dst_ref=r_ref.at[i, pl.ds(row * slab, slab)],
            send_sem=send_row.at[i, step], recv_sem=recv_row.at[i, step],
            device_id={"row": to}, device_id_type=MESH)

    def own_row_copy(i):
        return pltpu.make_async_copy(
            t_ref.at[i, row], r_ref.at[i, pl.ds(row * slab, slab)], own_row.at[i])

    def col_copy(i, step):
        to = partner(col, step, cols)
        return pltpu.make_async_remote_copy(
            src_ref=v_ref.at[i, to], dst_ref=w_ref.at[i, col],
            send_sem=send_col.at[i, step], recv_sem=recv_col.at[i, step],
            device_id={"col": to}, device_id_type=MESH)

    def own_col_copy(i):
        return pltpu.make_async_copy(v_ref.at[i, col], w_ref.at[i, col], own_col.at[i])

    tables[0].wait()
    span = rows * SUB
    arrived = set()
    for f in range(fields):
        for low_j, top_j in ((0, 1), (1, chunks)) if f == 0 else ((0, chunks),):
            for n in range(pieces):
                if (f, n) not in arrived:
                    load(f, n).wait()
                    arrived.add((f, n))
                high, low = halves(a_ref[f, n * width:(n + 1) * width, :])
                part = lax.dot_general(
                    hx_ref[low_j * span:top_j * span, :], jnp.concatenate([high, high, low], axis=1),
                    (((1,), (1,)), ((), ())), preferred_element_type=jnp.float32)
                part = part.reshape(top_j - low_j, rows, SUB, width)
                for j in range(low_j, top_j):
                    for b in range(per_dot):
                        at = (n * per_dot + b) * SUB
                        t_ref[f * chunks + j, :, at:at + SUB, :] = part[
                            j - low_j, :, :, b * LANES:(b + 1) * LANES]
            if not f and not low_j:
                pl.semaphore_wait(barrier, rows + cols - 2)
            for j in range(low_j, top_j):
                for step in range(rows - 1, 0, -1):
                    row_copy(f * chunks + j, step).start()
                own_row_copy(f * chunks + j).start()

    tables[1].wait()

    def y_step(i, carry):
        for step in range(rows - 1, 0, -1):
            row_copy(i, step).wait_recv()
        own_row_copy(i).wait()
        whole = []
        for q in range(quads):
            parts = [r_ref[i, pl.ds(q * groups + g, rows * blocks, stride=SUB), :] for g in range(groups)]
            whole.append(jnp.concatenate(swap_groups(parts), axis=0))
        high, low = halves(jnp.concatenate(whole, axis=1))
        got = jnp.dot(hy_ref[...], jnp.concatenate([high, high, low], axis=0),
                      preferred_element_type=jnp.float32)
        for c in range(cols):
            for q in range(quads):
                v_ref[i, c, q * share_y:(q + 1) * share_y, :] = got[
                    c * share_y:(c + 1) * share_y, q * LANES:(q + 1) * LANES]
        for step in range(cols - 1, 0, -1):
            col_copy(i, step).start()
        own_col_copy(i).start()
        return carry

    lax.fori_loop(0, total, y_step, 0)

    tables[2].wait()
    for n in range(ny // LANES):
        at = slice(n * LANES, (n + 1) * LANES)
        sy_rows[at, :] = jnp.broadcast_to(sy_ref[:, at], (LANES, LANES)).T

    def modes_of(i):
        for step in range(cols - 1, 0, -1):
            col_copy(i, step).wait_recv()
        own_col_copy(i).wait()
        lines = []
        for q in range(quads):
            tiles = []
            for c in range(0, cols, groups):
                tiles.append(swap_groups(
                    [w_ref[i, c + g, q * share_y:(q + 1) * share_y, :] for g in range(groups)]))
            for k in range(groups):
                lines.append(jnp.concatenate([tile[k] for tile in tiles], axis=1))
        high, low = halves(jnp.concatenate(lines, axis=0))
        got = jnp.dot(jnp.concatenate([high, low], axis=1), hz_ref[...],
                      preferred_element_type=jnp.float32)
        return got[:, :nz] + got[:, nz:]

    def z_step(i, carry):
        m_ref[i] = modes_of(i)
        return carry

    lax.fori_loop(0, total - chunks, z_step, 0)

    def last_step(j, carry):
        last = modes_of(total - chunks + j)
        lines_y = sy_rows[pl.ds(col * share_y, share_y), :]
        lines_y = jnp.concatenate([lines_y] * (nz // LANES), axis=1) + sz_ref[...]
        for k in range(SUB):
            at = slice(k * share_y, (k + 1) * share_y)
            weight = 1.0 / (1.0 + (sx_ref[row * (chunks * SUB) + j * SUB + k] + lines_y))
            old = [m_ref[f * chunks + j, at, :] for f in range(fields - 1)] + [last[at, :]]
            for f in range(fields):
                mixed = coupling_ref[f, 0] * old[0]
                for b in range(1, fields):
                    mixed = mixed + coupling_ref[f, b] * old[b]
                o_ref[f, j * SUB + k] = weight * old[f] + (1.0 - weight) * mixed
        return carry

    lax.fori_loop(0, chunks, last_step, 0)

    def drain(i, carry):
        for step in range(1, rows):
            row_copy(i, step).wait_send()
        for step in range(1, cols):
            col_copy(i, step).wait_send()
        return carry

    lax.fori_loop(0, total, drain, 0)


def local(rows, cols, species, coupling, symbol_x, symbol_y, symbol_z):
    fields, nx, near_y, near_z = species.shape
    ny, nz = near_y * rows, near_z * cols
    share_x, share_y = nx // rows, ny // cols
    groups = LANES // near_z
    blocks = near_y // groups
    total = fields * share_x // SUB

    order = np.arange(nx).reshape(rows, share_x // SUB, SUB).transpose(1, 0, 2).reshape(-1)
    high, low = halves_of(mode_table(nx)[order])
    hx = np.concatenate([high, low, high], axis=1)
    order = np.arange(ny).reshape(rows, blocks, groups).transpose(2, 0, 1).reshape(-1)
    high, low = halves_of(mode_table(ny)[:, order])
    hy = np.concatenate([high, low, high], axis=1)
    high, low = halves_of(mode_table(nz))
    hz = np.concatenate([np.concatenate([high, low], axis=1),
                         np.concatenate([high, np.zeros_like(low)], axis=1)], axis=0)

    lines = jnp.transpose(species, (0, 2, 3, 1)).reshape(fields, near_y * near_z, nx)
    vmem = pl.BlockSpec(memory_space=pltpu.VMEM)
    smem = pl.BlockSpec(memory_space=pltpu.SMEM)
    hbm = pl.BlockSpec(memory_space=pltpu.HBM)
    dma = pltpu.SemaphoreType.DMA
    f32 = jnp.float32
    chunks = total // fields
    return pl.pallas_call(
        functools.partial(kernel, (rows, cols, fields, nx, ny, nz)),
        out_shape=pltpu.VMEM((fields, share_x, share_y, nz), f32),
        in_specs=[smem, smem, hbm, hbm, hbm, hbm, vmem, vmem],
        out_specs=vmem,
        scratch_shapes=[
            pltpu.VMEM(lines.shape, f32),
            pltpu.VMEM(hx.shape, hx.dtype),
            pltpu.VMEM(hy.shape, hy.dtype),
            pltpu.VMEM(hz.shape, hz.dtype),
            pltpu.VMEM((ny, LANES), f32),
            pltpu.VMEM((max(total - chunks, 1), SUB * share_y, nz), f32),
            pltpu.VMEM((total, rows, blocks * SUB, LANES), f32),
            pltpu.VMEM((total, rows * blocks * SUB, LANES), f32),
            pltpu.VMEM((total, cols, SUB // groups * share_y, LANES), f32),
            pltpu.VMEM((total, cols, SUB // groups * share_y, LANES), f32),
            dma((fields, blocks // 2)), dma((3,)),
            dma((total, rows)), dma((total, rows)),
            dma((total, cols)), dma((total, cols)),
            dma((total,)), dma((total,)),
        ],
        compiler_params=pltpu.CompilerParams(
            collective_id=0, has_side_effects=True, vmem_limit_bytes=56 * 2**20),
    )(coupling, symbol_x, lines, jnp.asarray(hx), jnp.asarray(hy), jnp.asarray(hz),
      symbol_y[None, :], symbol_z[None, :])


def solution(mesh):
    return jax.shard_map(
        functools.partial(local, mesh.shape["row"], mesh.shape["col"]),
        mesh=mesh,
        in_specs=(P(None, None, "row", "col"), P(), P(), P(), P()),
        out_specs=P(None, "row", "col", None),
        check_vma=False,
    )
```

profile of v0, /device:TPU:0, one launch (start us, length us, event | category | flops | bytes accessed | tf_op | source)
XLA Modules:
  0.0 62.8 jit_solution(12696575255046528285)
XLA Ops:
  0.0 61.5 %shard_map.82 = f32[2,32,64,128]{3,2,1,0:T(8,128)S(1)} custom-call(f32[2,2]{1,0:T(2,128)} %coupling_ref.1, f32[256]{0:T(256)} %sx_ref.1, f32[2,1024,256]{2,1,0:T(8,128)} %bitcast.5, bf16[256,768]{1,0:T(8,128)(2,1)} %constant.6.clone.hx_hbm, bf16[256,768]{1,0:T(8,128)(2,1)} %constant.7.clone.hy_hbm, bf16[256,256]{1,0:T(8,128)(2,1)} %constant.8.clone.hz_hbm, ...), custom_call_target="tpu_custom_call" | custom-call | tf_op jit(solution)/shard_map/pallas_call | solution.py:249
  61.5 1.3 %copy.10 = f32[2,32,64,128]{3,2,1,0:T(8,128)} copy(f32[2,32,64,128]{3,2,1,0:T(8,128)S(1)} %shard_map.82) | data formatting | bytes 4194304
where the time goes:
time: 63 us; the launch traced here: 62.8 us
  Pallas kernels  61.5 us (98%)
  local copies, waits for them, and re-layouts  1.32 us (2%)
    pallas_call x1, Pallas kernels, local(): pl.pallas_call(functools.partial(kernel, (rows, cols, fields, nx, ny, nz)...  61.5 us
    unnamed x1, local copies, waits for them, and re-layouts  1.32 us

commit v1 on v0

v1 whole, which is shorter than its diff:
```python
import functools

import jax
import jax.numpy as jnp
import numpy as np
from jax import lax
from jax.experimental import pallas as pl
from jax.experimental.pallas import tpu as pltpu
from jax.sharding import PartitionSpec as P

MESH = pl.DeviceIdType.MESH
LANES = 128
SUB = 8
DEPTH = LANES // SUB
HELD = 4


def mode_table(count):
    rank = np.arange(1, count + 1)
    angle = np.pi / (count + 1) * ((rank[:, None] * rank[None, :]) % (2 * count + 2))
    return (np.sin(angle) * np.sqrt(2.0 / (count + 1))).astype(np.float32)


def halves_of(table):
    high = table.astype(jnp.bfloat16)
    low = (table - high.astype(np.float32)).astype(jnp.bfloat16)
    return high, low


def halves(values):
    high = values.astype(jnp.bfloat16)
    low = (values - high.astype(jnp.float32)).astype(jnp.bfloat16)
    return high, low


def partner(me, step, count):
    if count & (count - 1):
        return lax.rem(me + step, count)
    other, bit = me, 1
    while bit < count:
        if step & bit:
            other = other + bit * (1 - 2 * lax.rem(me // bit, 2))
        bit *= 2
    return other


def swap_groups(parts):
    parts = list(parts)
    count = len(parts)
    width = LANES // count
    lane = lax.broadcasted_iota(jnp.int32, parts[0].shape, 1)
    step = count // 2
    while step:
        keep = lax.rem(lane // (width * step), 2) == 0
        for first in range(count):
            if first & step:
                continue
            a, b = parts[first], parts[first + step]
            parts[first] = jnp.where(keep, a, pltpu.roll(b, width * step, 1))
            parts[first + step] = jnp.where(keep, pltpu.roll(a, LANES - width * step, 1), b)
        step //= 2
    return parts


def kernel(sizes, c_hbm, sx_hbm, a_hbm, hx_hbm, hy_hbm, hz_hbm, sy_hbm, sz_hbm, o_ref,
           c_ref, sx_ref, sy_ref, sz_ref, a_ref, hx_ref, hy_ref, hz_ref, sy_rows, m_ref,
           t_ref, r_ref, v_ref, w_ref,
           load_a, load_h, load_s, send_row, recv_row, send_col, recv_col):
    rows, cols, fields, nx, ny, nz = sizes
    share_y = ny // cols
    near_y = ny // rows
    depths = nz // cols // DEPTH
    blocks = near_y // SUB
    chunks = nx // rows // SUB
    stages = fields * depths
    total = stages * chunks
    slab = blocks * SUB
    span = rows * SUB
    row, col = lax.axis_index("row"), lax.axis_index("col")
    per_dot = 2
    width = per_dot * LANES
    pieces = blocks // per_dot

    def load(s, n):
        f, d = s // depths, s % depths
        lines = width // DEPTH
        return pltpu.make_async_copy(
            a_hbm.at[f, pl.ds(n * lines, lines), pl.ds(d * DEPTH, DEPTH)],
            a_ref.at[s, pl.ds(n * lines, lines)], load_a.at[s, n])

    tables = [pltpu.make_async_copy(src, dst, load_h.at[n]) for n, (src, dst) in enumerate(
        ((hx_hbm, hx_ref), (hy_hbm, hy_ref), (hz_hbm, hz_ref)))]
    smalls = [pltpu.make_async_copy(src, dst, load_s.at[n]) for n, (src, dst) in enumerate(
        ((c_hbm, c_ref), (sx_hbm, sx_ref), (sy_hbm, sy_ref), (sz_hbm, sz_ref)))]
    barrier = pltpu.get_barrier_semaphore()
    tables[0].start()
    for n in range(pieces):
        load(0, n).start()
    for step in range(1, rows):
        pl.semaphore_signal(barrier, inc=1, device_id={"row": partner(row, step, rows)}, device_id_type=MESH)
    for step in range(1, cols):
        pl.semaphore_signal(barrier, inc=1, device_id={"col": partner(col, step, cols)}, device_id_type=MESH)
    for s in range(1, stages):
        for n in range(pieces):
            load(s, n).start()
    tables[1].start()
    tables[2].start()
    for small in smalls:
        small.start()

    def row_copy(i, step):
        to = partner(row, step, rows)
        return pltpu.make_async_remote_copy(
            src_ref=t_ref.at[i, to], dst_ref=r_ref.at[i, pl.ds(row * slab, slab)],
            send_sem=send_row.at[0], recv_sem=recv_row.at[i],
            device_id={"row": to}, device_id_type=MESH)

    def col_copy(i, step):
        to = partner(col, step, cols)
        return pltpu.make_async_remote_copy(
            src_ref=v_ref.at[i, to], dst_ref=w_ref.at[i, col],
            send_sem=send_col.at[0], recv_sem=recv_col.at[i],
            device_id={"col": to}, device_id_type=MESH)

    def landed(ref, sem):
        pltpu.make_async_copy(ref, ref, sem).wait()

    def x_step(s, low_j, top_j, waits):
        for n in range(pieces):
            if waits:
                load(s, n).wait()
            lines = width // DEPTH
            high, low = halves(a_ref[s, n * lines:(n + 1) * lines].reshape(width, nx))
            part = lax.dot_general(
                hx_ref[low_j * span:top_j * span, :], jnp.concatenate([high, high, low], axis=1),
                (((1,), (1,)), ((), ())), preferred_element_type=jnp.float32)
            part = part.reshape(top_j - low_j, rows, SUB, width)
            for j in range(low_j, top_j):
                for b in range(per_dot):
                    at = (n * per_dot + b) * SUB
                    t_ref[s * chunks + j, :, at:at + SUB, :] = part[
                        j - low_j, :, :, b * LANES:(b + 1) * LANES]

    def x_send(s, low_j, top_j):
        for j in range(low_j, top_j):
            i = s * chunks + j
            for step in range(rows - 1, 0, -1):
                row_copy(i, step).start()
            r_ref[i, pl.ds(pl.multiple_of(row * slab, slab), slab), :] = t_ref[i, row]

    tables[0].wait()
    x_step(0, 0, 1, True)
    pl.semaphore_wait(barrier, rows + cols - 2)
    x_send(0, 0, 1)
    x_step(0, 1, chunks, False)
    x_send(0, 1, chunks)

    def x_stage(s, carry):
        x_step(s, 0, chunks, True)
        x_send(s, 0, chunks)
        return carry

    lax.fori_loop(1, stages, x_stage, 0)

    tables[1].wait()

    def held(step):
        to = partner(col, step, cols)
        late = jnp.logical_and(col * 2 >= cols, jnp.logical_and(to * 2 < cols, to * 4 >= cols))
        return jnp.where(late, HELD, 0)

    def col_send(i):
        for step in range(cols - 1, 0, -1):
            k = i - held(step)

            @pl.when(jnp.logical_and(k >= 0, k < total))
            def _():
                col_copy(k, step).start()

    def y_step(i, carry):
        landed(r_ref.at[i, pl.ds(0, (rows - 1) * slab)], recv_row.at[i])
        parts = [r_ref[i, pl.ds(g, rows * blocks, stride=SUB), :] for g in range(SUB)]
        high, low = halves(jnp.concatenate(swap_groups(parts), axis=0))
        got = jnp.dot(hy_ref[...], jnp.concatenate([high, high, low], axis=0),
                      preferred_element_type=jnp.float32)
        v_ref[i] = got.reshape(cols, share_y, LANES)
        col_send(i)
        w_ref[i, col] = v_ref[i, col]
        return carry

    lax.fori_loop(0, total, y_step, 0)

    def late_send(i, carry):
        col_send(i)
        return carry

    lax.fori_loop(total, total + HELD, late_send, 0)

    tables[2].wait()
    for small in smalls:
        small.wait()
    for n in range(ny // LANES):
        at = slice(n * LANES, (n + 1) * LANES)
        sy_rows[at, :] = jnp.broadcast_to(sy_ref[:, at], (LANES, LANES)).T

    def modes_of(f, j):
        parts = []
        for d in range(depths):
            i = (f * depths + d) * chunks + j
            landed(w_ref.at[i, pl.ds(0, cols - 1)], recv_col.at[i])
        tiles = []
        parts = [w_ref[(f * depths + p % depths) * chunks + j, p // depths] for p in range(cols * depths)]
        for p in range(0, cols * depths, SUB):
            tiles.append(swap_groups(parts[p:p + SUB]))
        lines = [jnp.concatenate([tile[k] for tile in tiles], axis=1) for k in range(SUB)]
        high, low = halves(jnp.concatenate(lines, axis=0))
        got = jnp.dot(jnp.concatenate([high, low], axis=1), hz_ref[...],
                      preferred_element_type=jnp.float32)
        return got[:, :nz] + got[:, nz:]

    def z_step(i, carry):
        m_ref[i] = modes_of(i // chunks, lax.rem(i, chunks))
        return carry

    lax.fori_loop(0, (fields - 1) * chunks, z_step, 0)

    def last_step(j, carry):
        last = modes_of(fields - 1, j)
        lines_y = sy_rows[pl.ds(col * share_y, share_y), :]
        lines_y = jnp.concatenate([lines_y] * (nz // LANES), axis=1) + sz_ref[...]
        for k in range(SUB):
            at = slice(k * share_y, (k + 1) * share_y)
            weight = 1.0 / (1.0 + (sx_ref[row * (chunks * SUB) + j * SUB + k] + lines_y))
            old = [m_ref[f * chunks + j, at, :] for f in range(fields - 1)] + [last[at, :]]
            for f in range(fields):
                mixed = c_ref[f, 0] * old[0]
                for b in range(1, fields):
                    mixed = mixed + c_ref[f, b] * old[b]
                o_ref[f, j * SUB + k] = weight * old[f] + (1.0 - weight) * mixed
        return carry

    lax.fori_loop(0, chunks, last_step, 0)

    landed(t_ref.at[pl.ds(0, total), pl.ds(0, rows - 1)], send_row.at[0])
    landed(v_ref.at[pl.ds(0, total), pl.ds(0, cols - 1)], send_col.at[0])


def local(rows, cols, species, coupling, symbol_x, symbol_y, symbol_z):
    fields, nx, near_y, near_z = species.shape
    ny, nz = near_y * rows, near_z * cols
    share_x, share_y = nx // rows, ny // cols
    depths, blocks, chunks = near_z // DEPTH, near_y // SUB, share_x // SUB
    stages = fields * depths
    total = stages * chunks

    order = np.arange(nx).reshape(rows, chunks, SUB).transpose(1, 0, 2).reshape(-1)
    high, low = halves_of(mode_table(nx)[order])
    hx = np.concatenate([high, low, high], axis=1)
    order = np.arange(ny).reshape(rows, blocks, SUB).transpose(2, 0, 1).reshape(-1)
    high, low = halves_of(mode_table(ny)[:, order])
    hy = np.concatenate([high, low, high], axis=1)
    high, low = halves_of(mode_table(nz))
    hz = np.concatenate([np.concatenate([high, low], axis=1),
                         np.concatenate([high, np.zeros_like(low)], axis=1)], axis=0)

    lines = jnp.transpose(species, (0, 2, 3, 1))
    vmem = pl.BlockSpec(memory_space=pltpu.VMEM)
    hbm = pl.BlockSpec(memory_space=pltpu.HBM)
    dma = pltpu.SemaphoreType.DMA
    f32 = jnp.float32
    return pl.pallas_call(
        functools.partial(kernel, (rows, cols, fields, nx, ny, nz)),
        out_shape=pltpu.VMEM((fields, share_x, share_y, nz), f32),
        in_specs=[hbm] * 8,
        out_specs=vmem,
        scratch_shapes=[
            pltpu.SMEM(coupling.shape, f32),
            pltpu.SMEM(symbol_x.shape, f32),
            pltpu.VMEM((1, ny), f32),
            pltpu.VMEM((1, nz), f32),
            pltpu.VMEM((stages, near_y, DEPTH, nx), f32),
            pltpu.VMEM(hx.shape, hx.dtype),
            pltpu.VMEM(hy.shape, hy.dtype),
            pltpu.VMEM(hz.shape, hz.dtype),
            pltpu.VMEM((ny, LANES), f32),
            pltpu.VMEM((max((fields - 1) * chunks, 1), SUB * share_y, nz), f32),
            pltpu.VMEM((total, rows, blocks * SUB, LANES), f32),
            pltpu.VMEM((total, rows * blocks * SUB, LANES), f32),
            pltpu.VMEM((total, cols, share_y, LANES), f32),
            pltpu.VMEM((total, cols, share_y, LANES), f32),
            dma((stages, blocks // 2)), dma((3,)), dma((4,)),
            dma((1,)), dma((total,)), dma((1,)), dma((total,)),
        ],
        compiler_params=pltpu.CompilerParams(
            collective_id=0, has_side_effects=True, vmem_limit_bytes=56 * 2**20),
    )(coupling, symbol_x, lines, jnp.asarray(hx), jnp.asarray(hy), jnp.asarray(hz),
      symbol_y[None, :], symbol_z[None, :])


def solution(mesh):
    return jax.shard_map(
        functools.partial(local, mesh.shape["row"], mesh.shape["col"]),
        mesh=mesh,
        in_specs=(P(None, None, "row", "col"), P(), P(), P(), P()),
        out_specs=P(None, "row", "col", None),
        check_vma=False,
    )
```

time: 63 us -> 57.2 us (0.908)
  the two profiles are of different devices: /device:TPU:0 before, /device:TPU:8 now
where the time goes in v1:
time: 57.2 us; the launch traced here: 57.1 us
  Pallas kernels  55.7 us (97%)
  local copies, waits for them, and re-layouts  1.32 us (2%)
    pallas_call x1, Pallas kernels, local(): pl.pallas_call(functools.partial(kernel, (rows, cols, fields, nx, ny, nz)...  55.7 us
    unnamed x1, local copies, waits for them, and re-layouts  1.32 us

profile of v1, /device:TPU:8, one launch (start us, length us, event | category | flops | bytes accessed | tf_op | source)
XLA Modules:
  0.0 57.1 jit_solution(5067037138684201691)
XLA Ops:
  0.0 55.7 %shard_map.82 = f32[2,32,64,128]{3,2,1,0:T(8,128)S(1)} custom-call(f32[2,2]{1,0:T(2,128)} %c_hbm.1, f32[256]{0:T(256)} %sx_hbm.1, f32[2,32,32,256]{3,2,1,0:T(8,128)} %bitcast.3, bf16[256,768]{1,0:T(8,128)(2,1)} %constant.6.clone.hx_hbm, bf16[256,768]{1,0:T(8,128)(2,1)} %constant.7.clone.hy_hbm, bf16[256,256]{1,0:T(8,128)(2,1)} %constant.8.clone.hz_hbm, ...), custom_call_target="tpu_custom_call" | custom-call | tf_op jit(solution)/shard_map/pallas_call | solution.py:271
  55.7 1.3 %copy.10 = f32[2,32,64,128]{3,2,1,0:T(8,128)} copy(f32[2,32,64,128]{3,2,1,0:T(8,128)S(1)} %shard_map.82) | data formatting | bytes 4194304

commit v2 on v1

v2 whole, which is shorter than its diff:
```python
import functools

import jax
import jax.numpy as jnp
import numpy as np
from jax import lax
from jax.experimental import pallas as pl
from jax.experimental.pallas import tpu as pltpu
from jax.sharding import PartitionSpec as P

MESH = pl.DeviceIdType.MESH
LANES = 128
SUB = 8
DEPTH = LANES // SUB
FIRST = 3
HELD = 5
RELAY = 4


def mode_table(count):
    rank = np.arange(1, count + 1)
    angle = np.pi / (count + 1) * ((rank[:, None] * rank[None, :]) % (2 * count + 2))
    return (np.sin(angle) * np.sqrt(2.0 / (count + 1))).astype(np.float32)


def halves_of(table):
    high = table.astype(jnp.bfloat16)
    low = (table - high.astype(np.float32)).astype(jnp.bfloat16)
    return high, low


def halves(values):
    high = values.astype(jnp.bfloat16)
    low = (values - high.astype(jnp.float32)).astype(jnp.bfloat16)
    return high, low


def partner(me, step, count):
    if count & (count - 1):
        return lax.rem(me + step, count)
    other, bit = me, 1
    while bit < count:
        if step & bit:
            other = other + bit * (1 - 2 * lax.rem(me // bit, 2))
        bit *= 2
    return other


def swap_groups(parts):
    parts = list(parts)
    count = len(parts)
    width = LANES // count
    lane = lax.broadcasted_iota(jnp.int32, parts[0].shape, 1)
    step = count // 2
    while step:
        keep = lax.rem(lane // (width * step), 2) == 0
        for first in range(count):
            if first & step:
                continue
            a, b = parts[first], parts[first + step]
            parts[first] = jnp.where(keep, a, pltpu.roll(b, width * step, 1))
            parts[first + step] = jnp.where(keep, pltpu.roll(a, LANES - width * step, 1), b)
        step //= 2
    return parts


def modes_of(f, j, chunks, depths, w_ref, hz_ref):
    cols, nz = w_ref.shape[1], hz_ref.shape[1] // 2
    parts = [w_ref[(f * depths + p % depths) * chunks + j, p // depths] for p in range(cols * depths)]
    tiles = [swap_groups(parts[p:p + SUB]) for p in range(0, cols * depths, SUB)]
    lines = [jnp.concatenate([tile[k] for tile in tiles], axis=1) for k in range(SUB)]
    high, low = halves(jnp.concatenate(lines, axis=0))
    got = jnp.dot(jnp.concatenate([high, low], axis=1), hz_ref[...],
                  preferred_element_type=jnp.float32)
    return got[:, :nz] + got[:, nz:]


def kernel(sizes, c_hbm, sx_hbm, a_hbm, hx_hbm, hy_hbm, hz_hbm, sy_hbm, sz_hbm,
           o_ref, g_ref, w_ref, hz_ref,
           c_ref, sx_ref, sy_ref, sz_ref, a_ref, hx_ref, hy_ref, sy_rows, m_ref,
           t_ref, r_ref, v_ref, q_ref, u_ref, x_ref,
           load_a, load_h, load_s, send_row, recv_row, send_col, recv_col, send_x, recv_x):
    rows, cols, fields, nx, ny, nz = sizes
    share_y = ny // cols
    near_y = ny // rows
    depths = nz // cols // DEPTH
    blocks = near_y // SUB
    chunks = nx // rows // SUB
    stages = fields * depths
    total = stages * chunks
    slab = blocks * SUB
    span = rows * SUB
    row, col = lax.axis_index("row"), lax.axis_index("col")
    chips, half = rows // 2, cols // 2
    chip, side = row // 2, lax.rem(row, 2)
    mirror = cols - 1 - col
    per_dot = 2
    width = per_dot * LANES
    pieces = blocks // per_dot

    def load(s, n):
        f, d = s // depths, s % depths
        lines = width // DEPTH
        return pltpu.make_async_copy(
            a_hbm.at[f, pl.ds(n * lines, lines), pl.ds(d * DEPTH, DEPTH)],
            a_ref.at[s, pl.ds(n * lines, lines)], load_a.at[s, n])

    tables = [pltpu.make_async_copy(src, dst, load_h.at[n]) for n, (src, dst) in enumerate(
        ((hx_hbm.at[pl.ds(0, span)], hx_ref.at[pl.ds(0, span)]),
         (hx_hbm.at[pl.ds(span, nx - span)], hx_ref.at[pl.ds(span, nx - span)]),
         (hy_hbm, hy_ref), (hz_hbm, hz_ref)))]
    smalls = [pltpu.make_async_copy(src, dst, load_s.at[n]) for n, (src, dst) in enumerate(
        ((c_hbm, c_ref), (sx_hbm, sx_ref), (sy_hbm, sy_ref), (sz_hbm, sz_ref)))]
    barrier = pltpu.get_barrier_semaphore()
    tables[0].start()
    for n in range(pieces):
        load(0, n).start()
    for step in range(1, rows):
        pl.semaphore_signal(barrier, inc=1, device_id={"row": partner(row, step, rows)}, device_id_type=MESH)
    for step in range(1, cols):
        pl.semaphore_signal(barrier, inc=1, device_id={"col": partner(col, step, cols)}, device_id_type=MESH)
    tables[1].start()
    for s in range(1, stages):
        for n in range(pieces):
            load(s, n).start()
    tables[2].start()
    tables[3].start()
    for small in smalls:
        small.start()

    def row_copy(i, to_chip, to_side):
        return pltpu.make_async_remote_copy(
            src_ref=t_ref.at[i, to_side, to_chip], dst_ref=r_ref.at[i, pl.ds(row * slab, slab)],
            send_sem=send_row.at[0], recv_sem=recv_row.at[i],
            device_id={"row": 2 * to_chip + to_side}, device_id_type=MESH)

    def cross_copy():
        return pltpu.make_async_remote_copy(
            src_ref=t_ref.at[0, 0], dst_ref=q_ref, send_sem=send_x.at[0], recv_sem=recv_x.at[0],
            device_id={"col": mirror}, device_id_type=MESH)

    def relay_copy(to_chip):
        return pltpu.make_async_remote_copy(
            src_ref=q_ref.at[to_chip], dst_ref=u_ref.at[pl.ds(row * slab, slab)],
            send_sem=send_x.at[1], recv_sem=recv_x.at[1],
            device_id={"row": 2 * to_chip}, device_id_type=MESH)

    def relay_col_copy(to):
        return pltpu.make_async_remote_copy(
            src_ref=x_ref.at[to], dst_ref=w_ref.at[0, mirror],
            send_sem=send_x.at[2], recv_sem=recv_x.at[2],
            device_id={"col": to}, device_id_type=MESH)

    def col_copy(i, step):
        to = partner(col, step, cols)
        return pltpu.make_async_remote_copy(
            src_ref=v_ref.at[i, to], dst_ref=w_ref.at[i, col],
            send_sem=send_col.at[0], recv_sem=recv_col.at[i],
            device_id={"col": to}, device_id_type=MESH)

    def landed(ref, sem):
        pltpu.make_async_copy(ref, ref, sem).wait()

    def x_step(s, low_j, top_j, waits):
        for n in range(pieces):
            if waits:
                load(s, n).wait()
            lines = width // DEPTH
            high, low = halves(a_ref[s, n * lines:(n + 1) * lines].reshape(width, nx))
            part = lax.dot_general(
                hx_ref[low_j * span:top_j * span, :], jnp.concatenate([high, high, low], axis=1),
                (((1,), (1,)), ((), ())), preferred_element_type=jnp.float32)
            part = part.reshape(top_j - low_j, 2, chips, SUB, width)
            for j in range(low_j, top_j):
                for b in range(per_dot):
                    at = (n * per_dot + b) * SUB
                    t_ref[s * chunks + j, :, :, at:at + SUB, :] = part[
                        j - low_j, :, :, :, b * LANES:(b + 1) * LANES]

    def x_send(s, low_j, top_j):
        for j in range(low_j, top_j):
            i = s * chunks + j
            for to_side in (1, 0):
                for step in range(chips - 1, 0, -1):
                    row_copy(i, partner(chip, step, chips), to_side).start()
                if low_j == 0 and top_j == 1 and to_side:
                    cross_copy().start()
            row_copy(i, chip, 1 - side).start()
            r_ref[i, pl.ds(pl.multiple_of(row * slab, slab), slab), :] = t_ref[i, side, chip]

    tables[0].wait()
    x_step(0, 0, 1, True)
    pl.semaphore_wait(barrier, rows + cols - 2)
    x_send(0, 0, 1)
    tables[1].wait()
    x_step(0, 1, chunks, False)
    x_send(0, 1, chunks)

    def x_stage(s, carry):
        x_step(s, 0, chunks, True)
        x_send(s, 0, chunks)
        return carry

    lax.fori_loop(1, stages, x_stage, 0)

    tables[2].wait()

    def crosses(step):
        return (partner(col, step, cols) // half) != (col // half)

    def held(step):
        to = partner(col, step, cols)
        late = jnp.logical_and(col * 2 >= cols, jnp.logical_and(to * 2 < cols, to * 4 >= cols))
        return jnp.where(late, HELD, 0)

    def col_send(i):
        for step in range(cols - 1, 0, -1):
            k = i - jnp.where(i < FIRST, 0, held(step))
            crossed = jnp.logical_and(jnp.logical_and(k == 0, side == 0), crosses(step))

            due = jnp.logical_and(jnp.logical_or(i < FIRST, k >= FIRST), k < total)

            @pl.when(jnp.logical_and(due, jnp.logical_not(crossed)))
            def _():
                col_copy(k, step).start()

    def y_modes(ref):
        parts = [ref[pl.ds(g, rows * blocks, stride=SUB), :] for g in range(SUB)]
        high, low = halves(jnp.concatenate(swap_groups(parts), axis=0))
        got = jnp.dot(hy_ref[...], jnp.concatenate([high, high, low], axis=0),
                      preferred_element_type=jnp.float32)
        return got.reshape(cols, share_y, LANES)

    def y_step(i, carry):
        landed(r_ref.at[i, pl.ds(0, (rows - 1) * slab)], recv_row.at[i])
        v_ref[i] = y_modes(r_ref.at[i])
        col_send(i)
        w_ref[i, col] = v_ref[i, col]
        return carry

    def late_send(i, carry):
        col_send(i)
        return carry

    lax.fori_loop(0, RELAY, y_step, 0)

    cross_copy().wait_recv()
    for step in range(chips - 1, 0, -1):
        relay_copy(partner(chip, step, chips)).start()

    @pl.when(side == 1)
    def _():
        relay_copy(chip).start()

    @pl.when(side == 0)
    def _():
        u_ref[pl.ds(pl.multiple_of(row * slab, slab), slab), :] = q_ref[chip]

    lax.fori_loop(RELAY, total, y_step, 0)

    lax.fori_loop(total, total + HELD, late_send, 0)

    @pl.when(side == 0)
    def _():
        landed(u_ref.at[pl.ds(0, (rows - 1) * slab)], recv_x.at[1])
        x_ref[...] = y_modes(u_ref)
        base = (col // half) * half
        for step in range(1, half):
            relay_col_copy(base + lax.rem(col - base + step, half)).start()
        w_ref[0, mirror] = x_ref[col]

    tables[3].wait()
    for small in smalls:
        small.wait()
    for n in range(ny // LANES):
        at = slice(n * LANES, (n + 1) * LANES)
        sy_rows[at, :] = jnp.broadcast_to(sy_ref[:, at], (LANES, LANES)).T

    def arrive(f, j):
        for d in range(depths):
            i = (f * depths + d) * chunks + j
            whole = jnp.logical_or(i > 0, side == 1)

            @pl.when(whole)
            def _():
                landed(w_ref.at[i, pl.ds(0, cols - 1)], recv_col.at[i])

            if half > 1:
                @pl.when(jnp.logical_not(whole))
                def _():
                    landed(w_ref.at[i, pl.ds(0, half - 1)], recv_col.at[i])
                    landed(w_ref.at[i, pl.ds(0, half - 1)], recv_x.at[2])

    def z_step(i, carry):
        f, j = i // chunks, lax.rem(i, chunks)
        arrive(f, j)
        m_ref[i] = modes_of(f, j, chunks, depths, w_ref, hz_ref)
        return carry

    lax.fori_loop(0, (fields - 1) * chunks, z_step, 0)

    def blend_step(x, carry):
        j, k = x // SUB, lax.rem(x, SUB)
        lines_y = sy_rows[pl.ds(pl.multiple_of(col * share_y, share_y), share_y), :]
        lines_y = jnp.concatenate([lines_y] * (nz // LANES), axis=1) + sz_ref[...]
        weight = 1.0 / (1.0 + (sx_ref[row * (chunks * SUB) + x] + lines_y))
        at = pl.ds(pl.multiple_of(k * share_y, share_y), share_y)
        old = [m_ref[f * chunks + j, at, :] for f in range(fields - 1)]
        for f in range(fields):
            gain = (1.0 - weight) * c_ref[f, fields - 1]
            g_ref[f, x] = gain if f < fields - 1 else weight + gain
            mixed = jnp.zeros_like(weight)
            for b in range(fields - 1):
                mixed = mixed + c_ref[f, b] * old[b]
            mixed = (1.0 - weight) * mixed
            o_ref[f, x] = weight * old[f] + mixed if f < fields - 1 else mixed
        return carry

    lax.fori_loop(0, chunks * SUB, blend_step, 0)

    def last_step(j, carry):
        arrive(fields - 1, j)
        last = modes_of(fields - 1, j, chunks, depths, w_ref, hz_ref)
        for k in range(SUB):
            for f in range(fields):
                x = j * SUB + k
                o_ref[f, x] = o_ref[f, x] + g_ref[f, x] * last[k * share_y:(k + 1) * share_y, :]
        return carry

    lax.fori_loop(0, chunks - 1, last_step, 0)
    arrive(fields - 1, chunks - 1)

    landed(t_ref.at[pl.ds(0, total), pl.ds(0, 1)], send_row.at[0])
    landed(t_ref.at[pl.ds(0, total), 1, pl.ds(0, chips - 1)], send_row.at[0])
    landed(v_ref.at[pl.ds(0, total - 1), pl.ds(0, cols - 1)], send_col.at[0])
    cross_copy().wait_send()
    landed(q_ref.at[pl.ds(0, chips - 1)], send_x.at[1])

    @pl.when(side == 1)
    def _():
        landed(v_ref.at[0, pl.ds(0, cols - 1)], send_col.at[0])
        landed(q_ref.at[0], send_x.at[1])

    if half > 1:
        @pl.when(side == 0)
        def _():
            landed(v_ref.at[0, pl.ds(0, half - 1)], send_col.at[0])
            landed(x_ref.at[pl.ds(0, half - 1)], send_x.at[2])


def finish(depths, o_ref, g_ref, w_ref, hz_ref, out_hbm, e_ref, sem):
    fields, share_x, share_y, nz = o_ref.shape
    ready = share_x - SUB
    early = [pltpu.make_async_copy(o_ref.at[f, pl.ds(0, ready)], out_hbm.at[f, pl.ds(0, ready)], sem.at[f])
             for f in range(fields)]
    for copy in early:
        copy.start()
    last = modes_of(fields - 1, share_x // SUB - 1, share_x // SUB, depths, w_ref, hz_ref)
    late = []
    for f in range(fields):
        for k in range(SUB):
            x = ready + k
            e_ref[f, k] = o_ref[f, x] + g_ref[f, x] * last[k * share_y:(k + 1) * share_y, :]
        late.append(pltpu.make_async_copy(e_ref.at[f], out_hbm.at[f, pl.ds(ready, SUB)], sem.at[fields + f]))
        late[-1].start()
    for copy in early + late:
        copy.wait()


def local(rows, cols, species, coupling, symbol_x, symbol_y, symbol_z):
    fields, nx, near_y, near_z = species.shape
    ny, nz = near_y * rows, near_z * cols
    share_x, share_y = nx // rows, ny // cols
    depths, blocks, chunks = near_z // DEPTH, near_y // SUB, share_x // SUB
    stages = fields * depths
    total = stages * chunks

    order = np.arange(nx).reshape(rows // 2, 2, chunks, SUB).transpose(2, 1, 0, 3).reshape(-1)
    high, low = halves_of(mode_table(nx)[order])
    hx = np.concatenate([high, low, high], axis=1)
    order = np.arange(ny).reshape(rows, blocks, SUB).transpose(2, 0, 1).reshape(-1)
    high, low = halves_of(mode_table(ny)[:, order])
    hy = np.concatenate([high, low, high], axis=1)
    high, low = halves_of(mode_table(nz))
    hz = np.concatenate([np.concatenate([high, low], axis=1),
                         np.concatenate([high, np.zeros_like(low)], axis=1)], axis=0)

    lines = jnp.transpose(species, (0, 2, 3, 1))
    vmem = pl.BlockSpec(memory_space=pltpu.VMEM)
    hbm = pl.BlockSpec(memory_space=pltpu.HBM)
    dma = pltpu.SemaphoreType.DMA
    f32 = jnp.float32
    out = (fields, share_x, share_y, nz)
    kept = 4 * (2 * fields * share_x * share_y * nz + total * cols * share_y * LANES) + 2 * hz.size
    held = pl.pallas_call(
        functools.partial(kernel, (rows, cols, fields, nx, ny, nz)),
        out_shape=[
            pltpu.VMEM(out, f32),
            pltpu.VMEM(out, f32),
            pltpu.VMEM((total, cols, share_y, LANES), f32),
            pltpu.VMEM(hz.shape, hz.dtype),
        ],
        in_specs=[hbm] * 8,
        out_specs=[vmem] * 4,
        scratch_shapes=[
            pltpu.SMEM(coupling.shape, f32),
            pltpu.SMEM(symbol_x.shape, f32),
            pltpu.VMEM((1, ny), f32),
            pltpu.VMEM((1, nz), f32),
            pltpu.VMEM((stages, near_y, DEPTH, nx), f32),
            pltpu.VMEM(hx.shape, hx.dtype),
            pltpu.VMEM(hy.shape, hy.dtype),
            pltpu.VMEM((ny, LANES), f32),
            pltpu.VMEM((max((fields - 1) * chunks, 1), SUB * share_y, nz), f32),
            pltpu.VMEM((total, 2, rows // 2, blocks * SUB, LANES), f32),
            pltpu.VMEM((total, rows * blocks * SUB, LANES), f32),
            pltpu.VMEM((total, cols, share_y, LANES), f32),
            pltpu.VMEM((rows // 2, blocks * SUB, LANES), f32),
            pltpu.VMEM((rows * blocks * SUB, LANES), f32),
            pltpu.VMEM((cols, share_y, LANES), f32),
            dma((stages, blocks // 2)), dma((4,)), dma((4,)),
            dma((1,)), dma((total,)), dma((1,)), dma((total,)), dma((3,)), dma((3,)),
        ],
        compiler_params=pltpu.CompilerParams(
            collective_id=0, has_side_effects=True, vmem_limit_bytes=60 * 2**20 - kept),
    )(coupling, symbol_x, lines, jnp.asarray(hx), jnp.asarray(hy), jnp.asarray(hz),
      symbol_y[None, :], symbol_z[None, :])
    return pl.pallas_call(
        functools.partial(finish, depths),
        out_shape=jax.ShapeDtypeStruct(out, f32),
        in_specs=[vmem] * 4,
        out_specs=hbm,
        scratch_shapes=[pltpu.VMEM((fields, SUB, share_y, nz), f32), dma((2 * fields,))],
        compiler_params=pltpu.CompilerParams(vmem_limit_bytes=16 * 2**20),
    )(*held)


def solution(mesh):
    return jax.shard_map(
        functools.partial(local, mesh.shape["row"], mesh.shape["col"]),
        mesh=mesh,
        in_specs=(P(None, None, "row", "col"), P(), P(), P(), P()),
        out_specs=P(None, "row", "col", None),
        check_vma=False,
    )
```

time: 57.2 us -> 55 us (0.962)
  local copies, waits for them, and re-layouts: 1.32 us -> 0 us
  Pallas kernels: 55.7 us -> 54.8 us
    pallas_call x1, Pallas kernels: 55.7 us -> 53.5 us  [local(): pl.pallas_call(functools.partial(kernel, (rows, cols, fields, nx, ny, nz)...]
    pallas_call x0 -> x1, Pallas kernels: none -> 1.34 us  [local(): pl.pallas_call(functools.partial(finish, depths), out_shape=jax.ShapeDtyp...]
    unnamed x1 -> x0, local copies, waits for them, and re-layouts: 1.32 us -> none
where the time goes in v2:
time: 55 us; the launch traced here: 54.8 us
  Pallas kernels  54.8 us (100%)
    pallas_call x1, Pallas kernels, local(): pl.pallas_call(functools.partial(kernel, (rows, cols, fields, nx, ny, nz)...  53.5 us
    pallas_call x1, Pallas kernels, local(): pl.pallas_call(functools.partial(finish, depths), out_shape=jax.ShapeDtyp...  1.34 us

profile of v2, /device:TPU:8, one launch (start us, length us, event | category | flops | bytes accessed | tf_op | source)
XLA Modules:
  0.0 54.8 jit_solution(151505565700206196)
XLA Ops:
  0.0 53.5 %shard_map.82 = (f32[2,32,64,128]{3,2,1,0:T(8,128)S(1)}, f32[2,32,64,128]{3,2,1,0:T(8,128)S(1)}, f32[16,4,64,128]{3,2,1,0:T(8,128)S(1)}, bf16[256,256]{1,0:T(8,128)(2,1)S(1)}) custom-call(f32[2,2]{1,0:T(2,128)} %c_hbm.1, f32[256]{0:T(256)} %sx_hbm.1, f32[2,32,32,256]{3,2,1,0:T(8,128)} %bitcast.3, bf16[256,768]{1,0:T(8,128)(2,1)} %constant.6.clone.hx_hbm, ...), custom_call_target="tpu_custom_call" | custom-call | tf_op jit(solution)/shard_map/pallas_call | solution.py:395
  53.5 1.3 %shard_map.83 = f32[2,32,64,128]{3,2,1,0:T(8,128)} custom-call(f32[2,32,64,128]{3,2,1,0:T(8,128)S(1)} %get-tuple-element.9.o_ref, f32[2,32,64,128]{3,2,1,0:T(8,128)S(1)} %get-tuple-element.10.g_ref, f32[16,4,64,128]{3,2,1,0:T(8,128)S(1)} %get-tuple-element.11.w_ref, bf16[256,256]{1,0:T(8,128)(2,1)S(1)} %get-tuple-element.12.hz_ref), custom_call_target="tpu_custom_call" | custom-call | tf_op jit(solution)/shard_map/pallas_call | solution.py:428

commit v3 on v2

--- a/solution.py
+++ b/solution.py
@@ -12,9 +12,9 @@
 LANES = 128
 SUB = 8
 DEPTH = LANES // SUB
-FIRST = 3
-HELD = 5
+HELD = 6
 RELAY = 4
+AHEAD = 2
 
 
 def mode_table(count):
@@ -94,6 +94,9 @@
     chips, half = rows // 2, cols // 2
     chip, side = row // 2, lax.rem(row, 2)
     mirror = cols - 1 - col
+    inner = jnp.logical_and(col * 4 >= cols, col * 4 < 3 * cols)
+    early = jnp.logical_or(side == 0, inner)
+    inners = half // 2
     per_dot = 2
     width = per_dot * LANES
     pieces = blocks // per_dot
@@ -119,14 +122,6 @@
         pl.semaphore_signal(barrier, inc=1, device_id={"row": partner(row, step, rows)}, device_id_type=MESH)
     for step in range(1, cols):
         pl.semaphore_signal(barrier, inc=1, device_id={"col": partner(col, step, cols)}, device_id_type=MESH)
-    tables[1].start()
-    for s in range(1, stages):
-        for n in range(pieces):
-            load(s, n).start()
-    tables[2].start()
-    tables[3].start()
-    for small in smalls:
-        small.start()
 
     def row_copy(i, to_chip, to_side):
         return pltpu.make_async_remote_copy(
@@ -134,21 +129,22 @@
             send_sem=send_row.at[0], recv_sem=recv_row.at[i],
             device_id={"row": 2 * to_chip + to_side}, device_id_type=MESH)
 
-    def cross_copy():
+    def cross_copy(to_side):
         return pltpu.make_async_remote_copy(
-            src_ref=t_ref.at[0, 0], dst_ref=q_ref, send_sem=send_x.at[0], recv_sem=recv_x.at[0],
+            src_ref=t_ref.at[0, to_side], dst_ref=q_ref.at[to_side],
+            send_sem=send_x.at[0], recv_sem=recv_x.at[2 + to_side],
             device_id={"col": mirror}, device_id_type=MESH)
 
-    def relay_copy(to_chip):
+    def relay_copy(to_chip, to_side):
         return pltpu.make_async_remote_copy(
-            src_ref=q_ref.at[to_chip], dst_ref=u_ref.at[pl.ds(row * slab, slab)],
-            send_sem=send_x.at[1], recv_sem=recv_x.at[1],
-            device_id={"row": 2 * to_chip}, device_id_type=MESH)
+            src_ref=q_ref.at[to_side, to_chip], dst_ref=u_ref.at[pl.ds(row * slab, slab)],
+            send_sem=send_x.at[1], recv_sem=recv_x.at[0],
+            device_id={"row": 2 * to_chip + to_side}, device_id_type=MESH)
 
     def relay_col_copy(to):
         return pltpu.make_async_remote_copy(
             src_ref=x_ref.at[to], dst_ref=w_ref.at[0, mirror],
-            send_sem=send_x.at[2], recv_sem=recv_x.at[2],
+            send_sem=send_x.at[2], recv_sem=recv_x.at[1],
             device_id={"col": to}, device_id_type=MESH)
 
     def col_copy(i, step):
@@ -177,33 +173,59 @@
                     t_ref[s * chunks + j, :, :, at:at + SUB, :] = part[
                         j - low_j, :, :, :, b * LANES:(b + 1) * LANES]
 
-    def x_send(s, low_j, top_j):
-        for j in range(low_j, top_j):
-            i = s * chunks + j
-            for to_side in (1, 0):
-                for step in range(chips - 1, 0, -1):
-                    row_copy(i, partner(chip, step, chips), to_side).start()
-                if low_j == 0 and top_j == 1 and to_side:
-                    cross_copy().start()
-            row_copy(i, chip, 1 - side).start()
-            r_ref[i, pl.ds(pl.multiple_of(row * slab, slab), slab), :] = t_ref[i, side, chip]
+    def row_send(i, to_side):
+        for step in range(chips - 1, 0, -1):
+            row_copy(i, partner(chip, step, chips), to_side).start()
+
+    def near_send(i):
+        row_copy(i, chip, 1 - side).start()
+        r_ref[i, pl.ds(pl.multiple_of(row * slab, slab), slab), :] = t_ref[i, side, chip]
+
+    def x_send(i):
+        row_send(i, 1)
+        row_send(i, 0)
+        near_send(i)
 
     tables[0].wait()
-    x_step(0, 0, 1, True)
+    for n in range(pieces):
+        load(0, n).wait()
+    tables[1].start()
+    for s in range(1, stages):
+        for n in range(pieces):
+            load(s, n).start()
+    tables[2].start()
+    tables[3].start()
+    for small in smalls:
+        small.start()
+    x_step(0, 0, 1, False)
     pl.semaphore_wait(barrier, rows + cols - 2)
-    x_send(0, 0, 1)
+    cross_copy(0).start()
+
+    @pl.when(inner)
+    def _():
+        cross_copy(1).start()
+
+    @pl.when(jnp.logical_not(inner))
+    def _():
+        row_send(0, 1)
+
+    near_send(0)
     tables[1].wait()
     x_step(0, 1, chunks, False)
-    x_send(0, 1, chunks)
+    for j in range(1, chunks):
+        x_send(j)
+    row_send(0, 0)
+
+    @pl.when(inner)
+    def _():
+        row_send(0, 1)
+
 
     def x_stage(s, carry):
         x_step(s, 0, chunks, True)
-        x_send(s, 0, chunks)
-        return carry
-
-    lax.fori_loop(1, stages, x_stage, 0)
-
-    tables[2].wait()
+        for j in range(chunks):
+            x_send(s * chunks + j)
+        return carry
 
     def crosses(step):
         return (partner(col, step, cols) // half) != (col // half)
@@ -213,12 +235,16 @@
         late = jnp.logical_and(col * 2 >= cols, jnp.logical_and(to * 2 < cols, to * 4 >= cols))
         return jnp.where(late, HELD, 0)
 
+    def turn(n):
+        return jnp.where(jnp.logical_and(early, n < chunks), lax.rem(n + 1, chunks), n)
+
     def col_send(i):
         for step in range(cols - 1, 0, -1):
-            k = i - jnp.where(i < FIRST, 0, held(step))
-            crossed = jnp.logical_and(jnp.logical_and(k == 0, side == 0), crosses(step))
-
-            due = jnp.logical_and(jnp.logical_or(i < FIRST, k >= FIRST), k < total)
+            n = i - jnp.where(i < chunks, 0, held(step))
+            k = turn(n)
+            crossed = jnp.logical_and(jnp.logical_and(k == 0, early), crosses(step))
+
+            due = jnp.logical_and(jnp.logical_or(i < chunks, n >= chunks), n < total)
 
             @pl.when(jnp.logical_and(due, jnp.logical_not(crossed)))
             def _():
@@ -232,37 +258,51 @@
         return got.reshape(cols, share_y, LANES)
 
     def y_step(i, carry):
-        landed(r_ref.at[i, pl.ds(0, (rows - 1) * slab)], recv_row.at[i])
-        v_ref[i] = y_modes(r_ref.at[i])
+        k = turn(i)
+        landed(r_ref.at[k, pl.ds(0, (rows - 1) * slab)], recv_row.at[k])
+        v_ref[k] = y_modes(r_ref.at[k])
         col_send(i)
-        w_ref[i, col] = v_ref[i, col]
+        w_ref[k, col] = v_ref[k, col]
         return carry
 
     def late_send(i, carry):
         col_send(i)
         return carry
 
-    lax.fori_loop(0, RELAY, y_step, 0)
-
-    cross_copy().wait_recv()
+    def x_y_stage(s, carry):
+        y_step(s - AHEAD, carry)
+        return x_stage(s, carry)
+
+    lax.fori_loop(1, AHEAD, x_stage, 0)
+    tables[2].wait()
+    lax.fori_loop(AHEAD, stages, x_y_stage, 0)
+    lax.fori_loop(stages - AHEAD, RELAY, y_step, 0)
+
+    cross_copy(0).wait_recv()
     for step in range(chips - 1, 0, -1):
-        relay_copy(partner(chip, step, chips)).start()
-
-    @pl.when(side == 1)
-    def _():
-        relay_copy(chip).start()
-
-    @pl.when(side == 0)
-    def _():
-        u_ref[pl.ds(pl.multiple_of(row * slab, slab), slab), :] = q_ref[chip]
+        relay_copy(partner(chip, step, chips), 0).start()
+
+    @pl.when(inner)
+    def _():
+        cross_copy(1).wait_recv()
+        for step in range(chips - 1, 0, -1):
+            relay_copy(partner(chip, step, chips), 1).start()
+
+    @pl.when(jnp.logical_or(side == 1, inner))
+    def _():
+        relay_copy(chip, 1 - side).start()
+
+    @pl.when(early)
+    def _():
+        u_ref[pl.ds(pl.multiple_of(row * slab, slab), slab), :] = q_ref[side, chip]
 
     lax.fori_loop(RELAY, total, y_step, 0)
 
     lax.fori_loop(total, total + HELD, late_send, 0)
 
-    @pl.when(side == 0)
-    def _():
-        landed(u_ref.at[pl.ds(0, (rows - 1) * slab)], recv_x.at[1])
+    @pl.when(early)
+    def _():
+        landed(u_ref.at[pl.ds(0, (rows - 1) * slab)], recv_x.at[0])
         x_ref[...] = y_modes(u_ref)
         base = (col // half) * half
         for step in range(1, half):
@@ -279,17 +319,23 @@
     def arrive(f, j):
         for d in range(depths):
             i = (f * depths + d) * chunks + j
-            whole = jnp.logical_or(i > 0, side == 1)
-
-            @pl.when(whole)
+
+            @pl.when(i > 0)
             def _():
                 landed(w_ref.at[i, pl.ds(0, cols - 1)], recv_col.at[i])
 
-            if half > 1:
-                @pl.when(jnp.logical_not(whole))
+            def first(near, far, on):
+                @pl.when(jnp.logical_and(i == 0, on))
                 def _():
-                    landed(w_ref.at[i, pl.ds(0, half - 1)], recv_col.at[i])
-                    landed(w_ref.at[i, pl.ds(0, half - 1)], recv_x.at[2])
+                    if near:
+                        landed(w_ref.at[i, pl.ds(0, near)], recv_col.at[i])
+                    if far:
+                        landed(w_ref.at[i, pl.ds(0, far)], recv_x.at[1])
+
+            first(half - 1, half - 1, side == 0)
+            odd = 2 * half - 1 - inners
+            first(odd, inners - 1, jnp.logical_and(side == 1, inner))
+            first(odd, inners, jnp.logical_and(side == 1, jnp.logical_not(inner)))
 
     def z_step(i, carry):
         f, j = i // chunks, lax.rem(i, chunks)
@@ -333,16 +379,24 @@
     landed(t_ref.at[pl.ds(0, total), pl.ds(0, 1)], send_row.at[0])
     landed(t_ref.at[pl.ds(0, total), 1, pl.ds(0, chips - 1)], send_row.at[0])
     landed(v_ref.at[pl.ds(0, total - 1), pl.ds(0, cols - 1)], send_col.at[0])
-    cross_copy().wait_send()
-    landed(q_ref.at[pl.ds(0, chips - 1)], send_x.at[1])
-
-    @pl.when(side == 1)
+    cross_copy(0).wait_send()
+    landed(q_ref.at[0, pl.ds(0, chips - 1)], send_x.at[1])
+
+    @pl.when(inner)
+    def _():
+        cross_copy(1).wait_send()
+        landed(q_ref.at[1, pl.ds(0, chips - 1)], send_x.at[1])
+
+    @pl.when(jnp.logical_or(side == 1, inner))
+    def _():
+        landed(q_ref.at[0, 0], send_x.at[1])
+
+    @pl.when(jnp.logical_not(early))
     def _():
         landed(v_ref.at[0, pl.ds(0, cols - 1)], send_col.at[0])
-        landed(q_ref.at[0], send_x.at[1])
 
     if half > 1:
-        @pl.when(side == 0)
+        @pl.when(early)
         def _():
             landed(v_ref.at[0, pl.ds(0, half - 1)], send_col.at[0])
             landed(x_ref.at[pl.ds(0, half - 1)], send_x.at[2])
@@ -415,11 +469,11 @@
             pltpu.VMEM((total, 2, rows // 2, blocks * SUB, LANES), f32),
             pltpu.VMEM((total, rows * blocks * SUB, LANES), f32),
             pltpu.VMEM((total, cols, share_y, LANES), f32),
-            pltpu.VMEM((rows // 2, blocks * SUB, LANES), f32),
+            pltpu.VMEM((2, rows // 2, blocks * SUB, LANES), f32),
             pltpu.VMEM((rows * blocks * SUB, LANES), f32),
             pltpu.VMEM((cols, share_y, LANES), f32),
             dma((stages, blocks // 2)), dma((4,)), dma((4,)),
-            dma((1,)), dma((total,)), dma((1,)), dma((total,)), dma((3,)), dma((3,)),
+            dma((1,)), dma((total,)), dma((1,)), dma((total,)), dma((3,)), dma((4,)),
         ],
         compiler_params=pltpu.CompilerParams(
             collective_id=0, has_side_effects=True, vmem_limit_bytes=60 * 2**20 - kept),

time: 55 us -> 54.8 us (level)
  no operation moved by 1% of the time
where the time goes in v3:
time: 54.8 us; the launch traced here: 54.6 us
  Pallas kernels  54.6 us (100%)
    pallas_call x1, Pallas kernels, local(): pl.pallas_call(functools.partial(kernel, (rows, cols, fields, nx, ny, nz)...  53.3 us
    pallas_call x1, Pallas kernels, local(): pl.pallas_call(functools.partial(finish, depths), out_shape=jax.ShapeDtyp...  1.34 us

profile of v3, /device:TPU:8, one launch (start us, length us, event | category | flops | bytes accessed | tf_op | source)
XLA Modules:
  0.0 54.6 jit_solution(4390908221598051089)
XLA Ops:
  0.0 53.3 %shard_map.82 = (f32[2,32,64,128]{3,2,1,0:T(8,128)S(1)}, f32[2,32,64,128]{3,2,1,0:T(8,128)S(1)}, f32[16,4,64,128]{3,2,1,0:T(8,128)S(1)}, bf16[256,256]{1,0:T(8,128)(2,1)S(1)}) custom-call(f32[2,2]{1,0:T(2,128)} %c_hbm.1, f32[256]{0:T(256)} %sx_hbm.1, f32[2,32,32,256]{3,2,1,0:T(8,128)} %bitcast.3, bf16[256,768]{1,0:T(8,128)(2,1)} %constant.6.clone.hx_hbm, ...), custom_call_target="tpu_custom_call" | custom-call | tf_op jit(solution)/shard_map/pallas_call | solution.py:449
  53.3 1.3 %shard_map.83 = f32[2,32,64,128]{3,2,1,0:T(8,128)} custom-call(f32[2,32,64,128]{3,2,1,0:T(8,128)S(1)} %get-tuple-element.9.o_ref, f32[2,32,64,128]{3,2,1,0:T(8,128)S(1)} %get-tuple-element.10.g_ref, f32[16,4,64,128]{3,2,1,0:T(8,128)S(1)} %get-tuple-element.11.w_ref, bf16[256,256]{1,0:T(8,128)(2,1)S(1)} %get-tuple-element.12.hz_ref), custom_call_target="tpu_custom_call" | custom-call | tf_op jit(solution)/shard_map/pallas_call | solution.py:482

commit v4 on v3

--- a/solution.py
+++ b/solution.py
@@ -181,9 +181,9 @@
         row_copy(i, chip, 1 - side).start()
         r_ref[i, pl.ds(pl.multiple_of(row * slab, slab), slab), :] = t_ref[i, side, chip]
 
-    def x_send(i):
-        row_send(i, 1)
-        row_send(i, 0)
+    def x_send(i, j):
+        row_send(i, j % 2)
+        row_send(i, 1 - j % 2)
         near_send(i)
 
     tables[0].wait()
@@ -213,7 +213,7 @@
     tables[1].wait()
     x_step(0, 1, chunks, False)
     for j in range(1, chunks):
-        x_send(j)
+        x_send(j, j)
     row_send(0, 0)
 
     @pl.when(inner)
@@ -224,7 +224,7 @@
     def x_stage(s, carry):
         x_step(s, 0, chunks, True)
         for j in range(chunks):
-            x_send(s * chunks + j)
+            x_send(s * chunks + j, j)
         return carry
 
     def crosses(step):

time: 54.8 us -> 54.7 us (level)
  no operation moved by 1% of the time
where the time goes in v4:
time: 54.7 us; the launch traced here: 54.5 us
  Pallas kernels  54.5 us (100%)
    pallas_call x1, Pallas kernels, local(): pl.pallas_call(functools.partial(kernel, (rows, cols, fields, nx, ny, nz)...  53.2 us
    pallas_call x1, Pallas kernels, local(): pl.pallas_call(functools.partial(finish, depths), out_shape=jax.ShapeDtyp...  1.34 us

profile of v4, /device:TPU:8, one launch (start us, length us, event | category | flops | bytes accessed | tf_op | source)
XLA Modules:
  0.0 54.5 jit_solution(5872765462758370321)
XLA Ops:
  0.0 53.2 %shard_map.82 = (f32[2,32,64,128]{3,2,1,0:T(8,128)S(1)}, f32[2,32,64,128]{3,2,1,0:T(8,128)S(1)}, f32[16,4,64,128]{3,2,1,0:T(8,128)S(1)}, bf16[256,256]{1,0:T(8,128)(2,1)S(1)}) custom-call(f32[2,2]{1,0:T(2,128)} %c_hbm.1, f32[256]{0:T(256)} %sx_hbm.1, f32[2,32,32,256]{3,2,1,0:T(8,128)} %bitcast.3, bf16[256,768]{1,0:T(8,128)(2,1)} %constant.6.clone.hx_hbm, ...), custom_call_target="tpu_custom_call" | custom-call | tf_op jit(solution)/shard_map/pallas_call | solution.py:449
  53.2 1.3 %shard_map.83 = f32[2,32,64,128]{3,2,1,0:T(8,128)} custom-call(f32[2,32,64,128]{3,2,1,0:T(8,128)S(1)} %get-tuple-element.9.o_ref, f32[2,32,64,128]{3,2,1,0:T(8,128)S(1)} %get-tuple-element.10.g_ref, f32[16,4,64,128]{3,2,1,0:T(8,128)S(1)} %get-tuple-element.11.w_ref, bf16[256,256]{1,0:T(8,128)(2,1)S(1)} %get-tuple-element.12.hz_ref), custom_call_target="tpu_custom_call" | custom-call | tf_op jit(solution)/shard_map/pallas_call | solution.py:482
